TPU v7x, 256 devices: a whole 4x4x8 slice. The times are simulated.
256 devices in a mesh: dp: 8 (over z_lo, core), cent: 32 (over y, z_hi, x).
Axes of the slice: x: 4, y: 4, z: 8 (z_hi: 2, z_lo: 4; z = z_hi * 4 + z_lo), core: 2. Of those that a mesh axis runs over, the one named last changes fastest.
Arguments:
- embeddings: bfloat16 [32768, 768], P(('dp', 'cent')), may hold values from -20 to 20
- fine_centroids: float32 [16384, 768], P('cent'), may hold values from -8 to 8
- parents: int32 [16384], P('cent'), may hold values from 0 to 2047
- coarse_centroids: float32 [2048, 768], P('cent'), may hold values from -6 to 6
Outputs:
- new_fine: float32 [16384, 768], P('cent')
- new_coarse: float32 [2048, 768], P('cent')
All inputs are finite; a program needn't handle non-finite values.
Results may differ from a plain program's by a relative error of at most 0.004.
Values may be sent and summed in bfloat16 or wider, within the bound.
No kernel may reach another device: no remote copies, remote signals or barrier semaphores. Data moves between devices by JAX's collectives and lax.ppermute only.
A program may use at most 64 MiB of HBM per device.

v0:
```python
import math
import jax
import jax.numpy as jnp
from jax import lax
from jax.sharding import PartitionSpec as P

KC = 2048
sharpness = 0.1
coarse_prior = 16.0


def copy_for_each(array, axis):
    devices = lax.axis_size(axis)
    return lax.all_to_all(
        jnp.broadcast_to(array[None], (devices, *array.shape)), axis, 0, 0, tiled=True
    )


def collected_together(array, axis):
    leaves = jax.tree.leaves(array)
    turns = sorted(range(len(leaves)), key=lambda k: -leaves[k].size)
    width = (1, *leaves[turns[0]].shape)[-1]
    lines = [
        jnp.pad(leaves[k].reshape(-1), (0, -leaves[k].size % width)).reshape(-1, width)
        for k in turns
    ]
    both, at, found = (copy_for_each(jnp.concatenate(lines), axis), 0, {})
    for k, line in zip(turns, lines):
        piece = both[:, at : at + len(line)].reshape(len(both), -1)
        found[k] = piece[:, : leaves[k].size].reshape(-1, *leaves[k].shape)
        at += len(line)
    numbers = iter(range(len(leaves)))
    return jax.tree.map(lambda _: found[next(numbers)], array)


def joined_by_halves(pieces, combine):
    while len(jax.tree.leaves(pieces)[0]) > 1:
        pieces = jax.vmap(combine)(
            *(jax.tree.map(lambda part: part[side::2], pieces) for side in (0, 1))
        )
    return jax.tree.map(lambda part: part[0], pieces)


def joined_all(array, axis, combine):
    pieces = collected_together(array, axis)
    return joined_by_halves(pieces, combine)


def cut_along(array, dim, devices):
    dims = array.shape
    tiles = array.reshape(*dims[:dim], devices, dims[dim] // devices, *dims[dim + 1 :])
    return jnp.moveaxis(tiles, dim, 0)


def summed_on_arrival(array, axis, dim):
    tiles = cut_along(array, dim, lax.axis_size(axis))
    arrived = lax.all_to_all(tiles, axis, split_axis=0, concat_axis=0, tiled=True)
    return arrived.sum(axis=0)


def side_by_side(arrays, axis, dim, along):
    widths = [math.prod(a.shape[along:]) for a in arrays]
    both = jnp.concatenate(
        [a.reshape(*a.shape[:along], w) for a, w in zip(arrays, widths)], axis=along
    )
    whole = summed_on_arrival(both, axis, dim)
    tiles = jnp.split(whole, [sum(widths[:k]) for k in range(1, len(widths))], axis=along)
    return tuple((b.reshape(*whole.shape[:along], *a.shape[along:]) for a, b in zip(arrays, tiles)))


def in_order(tiles, dim):
    dims = list(tiles.shape[1:])
    dims[dim] *= tiles.shape[0]
    return jnp.moveaxis(tiles, 0, dim).reshape(dims)


def gather_directly(array, axis, dim):
    tiles = copy_for_each(array, axis)
    return in_order(tiles, dim)


def block_logits(one_block, narrow_centroids, half_norm):
    scores = lax.dot_general(
        one_block, narrow_centroids, (((1,), (1,)), ((), ())), preferred_element_type=jnp.float32
    )
    return sharpness * (scores - half_norm[None, :])


def merge_stats(former, latter):
    highest = jnp.maximum(former[0], latter[0])
    combined = former[1] * jnp.exp(former[0] - highest) + latter[1] * jnp.exp(latter[0] - highest)
    return (highest, combined)


def coarse_terms(parent_ids, pooled, mass_rows):
    summed = jax.ops.segment_sum(pooled, parent_ids, num_segments=KC)
    weighted = jax.ops.segment_sum(mass_rows, parent_ids, num_segments=KC)
    return (summed, weighted)


def local(embeddings, fine_centroids, parents, coarse_centroids):
    gathered = lax.all_gather(embeddings, "cent", axis=0, tiled=True)
    row_count = gathered.shape[0]
    feat_width = gathered.shape[1]
    block_rows = math.gcd(row_count, 512)
    row_blocks = gathered.reshape(row_count // block_rows, block_rows, feat_width)
    narrow_centroids = fine_centroids.astype(jnp.bfloat16)
    half_norm = 0.5 * jnp.sum(fine_centroids * fine_centroids, axis=1)
    no_carry = jnp.zeros((), jnp.float32)

    def stats_step(carried, one_block):
        logits = block_logits(one_block, narrow_centroids, half_norm)
        highest = jnp.max(logits, axis=1)
        return (carried, (highest, jnp.sum(jnp.exp(logits - highest[:, None]), axis=1)))

    _, (local_peak, local_mass) = lax.scan(stats_step, no_carry, row_blocks)
    row_peak, row_mass = joined_all(
        (local_peak.reshape(-1), local_mass.reshape(-1)), "cent", merge_stats
    )

    def sum_step(carried, items):
        one_block, block_peak, block_mass = items
        logits = block_logits(one_block, narrow_centroids, half_norm)
        soft_weights = jnp.exp(logits - block_peak[:, None]) / block_mass[:, None]
        wide_block = one_block.astype(jnp.float32)
        summed = carried[0] + lax.dot_general(
            soft_weights,
            wide_block,
            (((0,), (0,)), ((), ())),
            precision=lax.Precision.HIGHEST,
            preferred_element_type=jnp.float32,
        )
        counted = carried[1] + jnp.sum(soft_weights, axis=0)
        return ((summed, counted), None)

    local_rows = fine_centroids.shape[0]
    start_state = (
        jnp.zeros(fine_centroids.shape, jnp.float32),
        jnp.zeros((local_rows,), jnp.float32),
    )
    stacked = (row_blocks, row_peak.reshape(-1, block_rows), row_mass.reshape(-1, block_rows))
    (fine_sums, fine_counts), _ = lax.scan(sum_step, start_state, stacked)
    total_sums, total_counts = lax.psum((fine_sums, fine_counts), "dp")
    pooled = fine_centroids + total_sums
    mass_rows = 1.0 + total_counts
    new_fine = pooled / mass_rows[:, None]
    col_width = feat_width // lax.axis_size("dp")
    first_col = lax.axis_index("dp") * col_width
    pooled_cols = lax.dynamic_slice_in_dim(pooled, first_col, col_width, 1)
    coarse_sum, coarse_mass = coarse_terms(parents, pooled_cols, mass_rows)
    owned_sum, owned_mass = side_by_side((coarse_sum, coarse_mass), "cent", 0, 1)
    old_cols = lax.dynamic_slice_in_dim(coarse_centroids, first_col, col_width, 1)
    new_cols = (coarse_prior * old_cols + owned_sum) / (coarse_prior + owned_mass)[:, None]
    new_coarse = gather_directly(new_cols, "dp", 1)
    return (new_fine, new_coarse)


def solution(mesh):
    in_specs = (P(("dp", "cent"), None), P("cent", None), P("cent"), P("cent", None))
    out_specs = (P("cent", None), P("cent", None))
    return jax.shard_map(local, mesh=mesh, in_specs=in_specs, out_specs=out_specs, check_vma=False)
```

profile of v0, /device:TPU:1, one launch (start us, length us, event | category | flops | bytes accessed | tf_op | source)
XLA Modules:
  0.0 385.6 jit_solution(6488801156989215922)
XLA Ops:
  7.9 2.2 multiply_reduce_fusion
  10.1 135.7 %all-gather.2.cloned.1.call-done = bf16[4096,768]{1,0:T(8,128)(2,1)} async-done(((bf16[128,768]{1,0:T(8,128)(2,1)}), bf16[4096,768]{1,0:T(8,128)(2,1)}) %all-gather.2.cloned.1.call-update) | async-done | bytes 6291472 | tf_op jit(solution)/shard_map/all_gather | solution.py:102
  145.9 16.8 %while.25 = (s32[]{:T(128)}, f32[8,512]{1,0:T(8,128)S(1)}, f32[8,512]{1,0:T(8,128)S(1)}, bf16[8,512,768]{2,1,0:T(8,128)(2,1)}, bf16[512,768]{1,0:T(8,128)(2,1)S(1)}, /*index=5*/f32[512]{0:T(512)S(1)}, s32[]{:T(128)}, s32[]{:T(128)}) while((s32[]{:T(128)}, f32[8,512]{1,0:T(8,128)S(1)}, f32[8,512]{1,0:T(8,128)S(1)}, ...), condition=%wide.region_4.5_spmd, body=%wide.region_1.4_spmd.sunk | while | flops 403962880 | bytes 3686505 | solution.py:116
  147.9 1.8 fusion.36
  150.0 1.8 fusion.36
  152.1 1.8 fusion.36
  164.2 5.3 %all-to-all-start = ((f32[32,2,4096]{2,1,0:T(2,128)}), f32[32,2,4096]{2,1,0:T(2,128)S(1)}, u32[]{:S(2)}, u32[]{:S(2)}) async-start(f32[32,2,4096]{2,1,0:T(2,128)} %broadcast_in_dim.44), calls=%async_computation | async-start | bytes 2097152 | tf_op jit(solution)/shard_map/all_to_all | solution.py:14
  169.5 18.9 %all-to-all-done = f32[32,2,4096]{2,1,0:T(2,128)S(1)} async-done(((f32[32,2,4096]{2,1,0:T(2,128)}), f32[32,2,4096]{2,1,0:T(2,128)S(1)}, u32[]{:S(2)}, u32[]{:S(2)}) %all-to-all-start) | async-done | bytes 1048608 | tf_op jit(solution)/shard_map/all_to_all | solution.py:14
  192.7 40.9 %while.26 = (s32[]{:T(128)}, f32[512,768]{1,0:T(8,128)S(1)}, f32[512]{0:T(512)S(1)}, bf16[8,512,768]{2,1,0:T(8,128)(2,1)}, bf16[512,768]{1,0:T(8,128)(2,1)S(1)},...) while((s32[]{:T(128)}, f32[512,768]{1,0:T(8,128)S(1)}, ...), condition=%wide.region_7.8_spmd.clone, body=%wide.region_5.7_spmd.clone.sunk | while | flops 2820669952 | bytes 7624836 | solution.py:142
  192.7 1.9 fusion.40
  194.6 3.2 select_add_fusion.4
  197.8 1.9 fusion.40
  199.7 3.2 select_add_fusion.4
  202.9 1.9 fusion.40
  204.8 3.2 select_add_fusion.4
  208.0 1.9 fusion.40
  209.9 3.2 select_add_fusion.4
  213.2 1.9 fusion.40
  215.0 3.2 select_add_fusion.4
  218.3 1.9 fusion.40
  220.2 3.2 select_add_fusion.4
  223.4 1.9 fusion.40
  225.3 3.2 select_add_fusion.4
  228.5 1.9 fusion.40
  230.4 3.2 select_add_fusion.4
  234.8 22.7 %psum.15 = f32[512]{0:T(512)S(1)} all-reduce(f32[512]{0:T(512)S(1)} %get-tuple-element.81), channel_id=1, replica_groups=mesh['dp'=8,'cent'=32] {'dp'}, use_global_device_ids=true, to_apply=%region_9.10 | all-reduce | flops 512 | bytes 4096 | tf_op jit(solution)/shard_map/psum | solution.py:143
  257.5 3.4 scatter_custom_fusion.1
  261.8 56.3 %all-reduce.2.cloned.1.call-done = f32[512,768]{1,0:T(8,128)} async-done(((f32[512,768]{1,0:T(8,128)}), f32[512,768]{1,0:T(8,128)}) %all-reduce.2.cloned.1.call-update) | async-done | bytes 1572880 | tf_op jit(solution)/shard_map/psum | solution.py:143
  318.1 3.3 broadcast_divide_fusion
  321.4 3.1 scatter_custom_fusion
  324.9 36.6 %all_to_all.15 = f32[32,64,97]{2,1,0:T(8,128)S(1)} all-to-all(f32[32,64,97]{2,1,0:T(8,128)S(1)} %pad_maximum_fusion), channel_id=1, replica_groups=mesh['dp'=8,'cent'=32] {'cent'}, dimensions={0} | all-to-all | bytes 1589248 | tf_op jit(solution)/shard_map/all_to_all | solution.py:57
  362.8 15.0 %all_to_all.16 = f32[8,64,96]{2,1,0:T(8,128)S(1)} all-to-all(f32[8,64,96]{2,1,0:T(8,128)S(1)} %broadcast_in_dim.48), channel_id=1, replica_groups=mesh['dp'=8,'cent'=32] {'dp'}, dimensions={0} | all-to-all | bytes 393216 | tf_op jit(solution)/shard_map/all_to_all | solution.py:14
  (100 shorter events, 22.3 us)
Async XLA Ops:
  7.2 138.7 %all-gather.2.cloned.1.call-start = ((), (), s32[]{:S(2)}) async-start(), calls=%async_computation.3 | async-start | bytes 6488064 | tf_op jit(solution)/shard_map/all_gather | solution.py:102
  162.6 1.5 copy-start.2
  164.2 24.2 %all-to-all-start = ((f32[32,2,4096]{2,1,0:T(2,128)}), f32[32,2,4096]{2,1,0:T(2,128)S(1)}, u32[]{:S(2)}, u32[]{:S(2)}) async-start(f32[32,2,4096]{2,1,0:T(2,128)} %broadcast_in_dim.44), calls=%async_computation | async-start | bytes 2097152 | tf_op jit(solution)/shard_map/all_to_all | solution.py:14
  169.4 148.7 %all-reduce.2.cloned.1.call-start = ((), (), s32[]{:S(2)}) async-start(), calls=%async_computation.4 | async-start | bytes 3145728 | tf_op jit(solution)/shard_map/psum | solution.py:143
  191.0 1.6 copy-start.3
  233.6 1.1 copy-start
  233.6 84.5 %copy-start.1 = (f32[512,768]{1,0:T(8,128)S(1)}, f32[512,768]{1,0:T(8,128)}, u32[]{:S(2)}) copy-start(f32[512,768]{1,0:T(8,128)} %param.9) | copy-start | bytes 4718596
Sparse Core Ops, SparseCore 0:
  11.4 134.4 all-gather.1
  234.9 83.1 all-reduce.1
where the time goes:
time: 387 us; the launch traced here: 386 us
  waiting for transfers between devices  212 us (55%)
  blocking collectives  74.4 us (19%)
  matrix products  54.4 us (14%)
  other arithmetic  15.7 us (4%)
  between operations  14.4 us (4%)
  local copies, waits for them, and re-layouts  9.1 us (2%)
  starting transfers between devices  5.35 us (1%)
    all_gather x1, waiting for transfers between devices, local(): gathered = lax.all_gather(embeddings, 'cent', axis=0, tiled=True)  136 us
    psum x1, waiting for transfers between devices, local(): total_sums, total_counts = lax.psum((fine_sums, fine_counts), 'dp')  56.3 us
    all_to_all x1, blocking collectives, summed_on_arrival(): lax.all_to_all(tiles, axis, split_axis=0, concat_axis=0, tiled=True)  36.6 us
    dot_general x16, matrix products, block_logits(): lax.dot_general(one_block, narrow_centroids, (((1,), (1,)), ((), ())), pr...  29 us
    dot_general x8, matrix products, sum_step(): lax.dot_general(soft_weights, wide_block, (((0,), (0,)), ((), ())), preci...  25.5 us
    psum x1, blocking collectives, local(): total_sums, total_counts = lax.psum((fine_sums, fine_counts), 'dp')  22.7 us
    all_to_all x1, waiting for transfers between devices, copy_for_each(): lax.all_to_all(jnp.broadcast_to(array[None], (devices, *array.shape)), ax...  18.9 us
    all_to_all x1, blocking collectives, copy_for_each(): lax.all_to_all(jnp.broadcast_to(array[None], (devices, *array.shape)), ax...  15 us
  transfers between devices with their start and end apart: 3, of which 3 were waited for; matrix products, arithmetic and copies ran while one was open for 2% of the time, Pallas kernels for 0%

commit v1 on v0

--- a/solution.py
+++ b/solution.py
@@ -99,7 +99,9 @@
 
 
 def local(embeddings, fine_centroids, parents, coarse_centroids):
-    gathered = lax.all_gather(embeddings, "cent", axis=0, tiled=True)
+    small = jnp.stack(lax.axis_size("cent") * [embeddings])
+    all_values = lax.all_to_all(small, "cent", 0, 0)
+    gathered = jnp.concatenate(all_values, axis=0)
     row_count = gathered.shape[0]
     feat_width = gathered.shape[1]
     block_rows = math.gcd(row_count, 512)

time: 387 us -> 418 us (1.080)
  waiting for transfers between devices: 212 us -> 157 us
  starting transfers between devices: 5.35 us -> 55.5 us
  blocking collectives: 74.4 us -> 108 us
  local copies, waits for them, and re-layouts: 9.1 us -> 13.4 us
    all_gather x1 -> x0, waiting for transfers between devices: 136 us -> none  [local(): gathered = lax.all_gather(embeddings, 'cent', axis=0, tiled=True)]
    all_to_all x0 -> x1, waiting for transfers between devices: none -> 87.9 us  [local(): all_values = lax.all_to_all(small, 'cent', 0, 0)]
    all_to_all x1, starting transfers between devices: 5.27 us -> 40.8 us  [copy_for_each(): lax.all_to_all(jnp.broadcast_to(array[None], (devices, *array.shape)), ax...]
    psum x1, blocking collectives: 22.7 us -> 56.4 us  [local(): total_sums, total_counts = lax.psum((fine_sums, fine_counts), 'dp')]
    all_to_all x0 -> x1, starting transfers between devices: none -> 14.7 us  [local(): all_values = lax.all_to_all(small, 'cent', 0, 0)]
    another operation x0 -> x1, local copies, waits for them, and re-layouts: none -> 4.3 us  [local(): small = jnp.stack(lax.axis_size('cent') * [embeddings])]
  transfers between devices with their start and end apart: 3 -> 3, of which waited for: 3 -> 3; matrix products, arithmetic and copies ran while one was open for 2% -> 1% of each run, Pallas kernels for 0% -> 0%
where the time goes in v1:
time: 418 us; the launch traced here: 417 us
  waiting for transfers between devices  157 us (38%)
  blocking collectives  108 us (26%)
  starting transfers between devices  55.5 us (13%)
  matrix products  54 us (13%)
  between operations  14.4 us (3%)
  other arithmetic  13.8 us (3%)
  local copies, waits for them, and re-layouts  13.4 us (3%)
    all_to_all x1, waiting for transfers between devices, local(): all_values = lax.all_to_all(small, 'cent', 0, 0)  87.9 us
    psum x1, blocking collectives, local(): total_sums, total_counts = lax.psum((fine_sums, fine_counts), 'dp')  56.4 us
    psum x1, waiting for transfers between devices, local(): total_sums, total_counts = lax.psum((fine_sums, fine_counts), 'dp')  54.1 us
    all_to_all x1, starting transfers between devices, copy_for_each(): lax.all_to_all(jnp.broadcast_to(array[None], (devices, *array.shape)), ax...  40.8 us
    all_to_all x1, blocking collectives, summed_on_arrival(): lax.all_to_all(tiles, axis, split_axis=0, concat_axis=0, tiled=True)  36.6 us
    dot_general x16, matrix products, block_logits(): lax.dot_general(one_block, narrow_centroids, (((1,), (1,)), ((), ())), pr...  29 us
    dot_general x8, matrix products, sum_step(): lax.dot_general(soft_weights, wide_block, (((0,), (0,)), ((), ())), preci...  25 us
    all_to_all x1, blocking collectives, copy_for_each(): lax.all_to_all(jnp.broadcast_to(array[None], (devices, *array.shape)), ax...  15 us
  transfers between devices with their start and end apart: 3, of which 3 were waited for; matrix products, arithmetic and copies ran while one was open for 1% of the time, Pallas kernels for 0%

profile of v1, /device:TPU:1, one launch (start us, length us, event | category | flops | bytes accessed | tf_op | source)
XLA Modules:
  0.0 416.6 jit_solution(7228256148137498698)
XLA Ops:
  7.2 4.3 %stack.2 = bf16[32,128,768]{2,1,0:T(8,128)(2,1)} broadcast(bf16[128,768]{1,0:T(8,128)(2,1)} %param.8), dimensions={1,2} | broadcast | bytes 6488064 | tf_op jit(solution)/shard_map/stack | solution.py:102
  11.5 14.7 %all-to-all-start = ((bf16[32,128,768]{2,1,0:T(8,128)(2,1)}), bf16[32,128,768]{2,1,0:T(8,128)(2,1)}, u32[]{:S(2)}, u32[]{:S(2)}) async-start(bf16[32,128,768]{2,1,0:T(8,128)(2,1)} %stack.2), calls=%async_computation | async-start | bytes 12582912 | tf_op jit(solution)/shard_map/all_to_all | solution.py:103
  26.4 87.9 %all-to-all-done = bf16[32,128,768]{2,1,0:T(8,128)(2,1)} async-done(((bf16[32,128,768]{2,1,0:T(8,128)(2,1)}), bf16[32,128,768]{2,1,0:T(8,128)(2,1)}, u32[]{:S(2)}, u32[]{:S(2)}) %all-to-all-start) | async-done | bytes 6291488 | tf_op jit(solution)/shard_map/all_to_all | solution.py:103
  114.3 16.8 %while.25 = (s32[]{:T(128)}, f32[8,512]{1,0:T(8,128)S(1)}, f32[8,512]{1,0:T(8,128)S(1)}, bf16[8,512,768]{2,1,0:T(8,128)(2,1)}, bf16[512,768]{1,0:T(8,128)(2,1)S(1)}, /*index=5*/f32[512]{0:T(512)S(1)}, s32[]{:T(128)}, s32[]{:T(128)}) while((s32[]{:T(128)}, f32[8,512]{1,0:T(8,128)S(1)}, f32[8,512]{1,0:T(8,128)S(1)}, ...), condition=%wide.region_4.5_spmd, body=%wide.region_1.4_spmd.sunk | while | flops 403962880 | bytes 3687005 | solution.py:118
  114.3 1.8 fusion.36
  116.4 1.8 fusion.36
  132.7 40.8 %all-to-all-start.1 = ((f32[32,2,4096]{2,1,0:T(2,128)}), f32[32,2,4096]{2,1,0:T(2,128)S(1)}, u32[]{:S(2)}, u32[]{:S(2)}) async-start(f32[32,2,4096]{2,1,0:T(2,128)} %broadcast_in_dim.44), calls=%async_computation.1 | async-start | bytes 2097152 | tf_op jit(solution)/shard_map/all_to_all | solution.py:14
  173.5 14.8 %all-to-all-done.1 = f32[32,2,4096]{2,1,0:T(2,128)S(1)} async-done(((f32[32,2,4096]{2,1,0:T(2,128)}), f32[32,2,4096]{2,1,0:T(2,128)S(1)}, u32[]{:S(2)}, u32[]{:S(2)}) %all-to-all-start.1) | async-done | bytes 1048608 | tf_op jit(solution)/shard_map/all_to_all | solution.py:14
  192.6 40.5 %while.26 = (s32[]{:T(128)}, f32[512,768]{1,0:T(8,128)S(1)}, f32[512]{0:T(512)S(1)}, bf16[8,512,768]{2,1,0:T(8,128)(2,1)}, bf16[512,768]{1,0:T(8,128)(2,1)S(1)},...) while((s32[]{:T(128)}, f32[512,768]{1,0:T(8,128)S(1)}, ...), condition=%wide.region_7.8_spmd.clone, body=%wide.region_5.7_spmd.clone.sunk | while | flops 2820669952 | bytes 7625844 | solution.py:144
  192.6 1.9 fusion.40
  194.5 3.1 select_add_fusion.4
  197.6 1.9 fusion.40
  199.5 3.1 select_add_fusion.4
  202.7 1.9 fusion.40
  204.6 3.1 select_add_fusion.4
  207.8 1.9 fusion.40
  209.7 3.1 select_add_fusion.4
  212.8 1.9 fusion.40
  214.7 3.1 select_add_fusion.4
  217.9 1.9 fusion.40
  219.8 3.1 select_add_fusion.4
  223.0 1.9 fusion.40
  224.8 3.1 select_add_fusion.4
  228.0 1.9 fusion.40
  229.9 3.1 select_add_fusion.4
  234.2 56.4 %psum.15 = f32[512]{0:T(512)S(1)} all-reduce(f32[512]{0:T(512)S(1)} %get-tuple-element.81), channel_id=1, replica_groups=mesh['dp'=8,'cent'=32] {'dp'}, use_global_device_ids=true, to_apply=%region_9.10 | all-reduce | flops 512 | bytes 4096 | tf_op jit(solution)/shard_map/psum | solution.py:145
  290.6 3.6 scatter_custom_fusion.1
  295.1 54.1 %all-reduce.2.cloned.1.call-done = f32[512,768]{1,0:T(8,128)} async-done(((f32[512,768]{1,0:T(8,128)}), f32[512,768]{1,0:T(8,128)}) %all-reduce.2.cloned.1.call-update) | async-done | bytes 1572880 | tf_op jit(solution)/shard_map/psum | solution.py:145
  349.1 3.3 broadcast_divide_fusion
  352.4 3.1 scatter_custom_fusion
  355.9 36.6 %all_to_all.20 = f32[32,64,97]{2,1,0:T(8,128)S(1)} all-to-all(f32[32,64,97]{2,1,0:T(8,128)S(1)} %pad_maximum_fusion), channel_id=1, replica_groups=mesh['dp'=8,'cent'=32] {'cent'}, dimensions={0} | all-to-all | bytes 1589248 | tf_op jit(solution)/shard_map/all_to_all | solution.py:57
  393.8 15.0 %all_to_all.21 = f32[8,64,96]{2,1,0:T(8,128)S(1)} all-to-all(f32[8,64,96]{2,1,0:T(8,128)S(1)} %broadcast_in_dim.48), channel_id=1, replica_groups=mesh['dp'=8,'cent'=32] {'dp'}, dimensions={0} | all-to-all | bytes 393216 | tf_op jit(solution)/shard_map/all_to_all | solution.py:14
  (102 shorter events, 23.5 us)
Async XLA Ops:
  11.5 14.8 %copy-start.1 = (f32[512,768]{1,0:T(8,128)S(1)}, f32[512,768]{1,0:T(8,128)}, u32[]{:S(2)}) copy-start(f32[512,768]{1,0:T(8,128)} %param.9) | copy-start | bytes 4718596
  11.5 102.9 %all-to-all-start = ((bf16[32,128,768]{2,1,0:T(8,128)(2,1)}), bf16[32,128,768]{2,1,0:T(8,128)(2,1)}, u32[]{:S(2)}, u32[]{:S(2)}) async-start(bf16[32,128,768]{2,1,0:T(8,128)(2,1)} %stack.2), calls=%async_computation | async-start | bytes 12582912 | tf_op jit(solution)/shard_map/all_to_all | solution.py:103
  131.1 1.5 copy-start.3
  132.7 55.7 %all-to-all-start.1 = ((f32[32,2,4096]{2,1,0:T(2,128)}), f32[32,2,4096]{2,1,0:T(2,128)S(1)}, u32[]{:S(2)}, u32[]{:S(2)}) async-start(f32[32,2,4096]{2,1,0:T(2,128)} %broadcast_in_dim.44), calls=%async_computation.1 | async-start | bytes 2097152 | tf_op jit(solution)/shard_map/all_to_all | solution.py:14
  173.4 175.7 %all-reduce.2.cloned.1.call-start = ((), (), s32[]{:S(2)}) async-start(), calls=%async_computation.4 | async-start | bytes 3145728 | tf_op jit(solution)/shard_map/psum | solution.py:145
  190.9 1.6 copy-start.4
  233.1 1.1 copy-start
  233.1 116.1 %copy-start.2 = (f32[512,768]{1,0:T(8,128)S(1)}, f32[512,768]{1,0:T(8,128)}, u32[]{:S(2)}) copy-start(f32[512,768]{1,0:T(8,128)} %param.9) | copy-start | bytes 4718596
Sparse Core Ops, SparseCore 0:
  234.3 114.7 all-reduce.1
